TPU v7x, 256 devices: a whole 4x4x8 slice. The times are simulated.
256 devices in a mesh: row: 4 (over z_hi, core), col: 16 (over z_lo, y), layer: 4 (over x).
Axes of the slice: x: 4, y: 4, z: 8 (z_hi: 2, z_lo: 4; z = z_hi * 4 + z_lo), core: 2. Of those that a mesh axis runs over, the one named last changes fastest.
Arguments:
- amplitudes: float32 [2016, 73536], P('row', ('layer', 'col')), may hold values from -6 to 6
- integrals: float32 [73536, 768], P(('layer', 'col'), 'row'), may hold values from -0.0625 to 0.0625
- occ_energy: float32 [64], replicated, may hold values from -2 to -0.5
- vir_energy: float32 [384], replicated, may hold values from 0.2 to 3
Outputs:
- ladder: float32 [2016, 768], P('col', ('row', 'layer'))
- amplitude_step: float32 [2016, 768], P('col', ('row', 'layer'))
All inputs are finite; a program needn't handle non-finite values.
Results may differ from a plain program's by a relative error of at most 0.00007.
Values sent between devices are 32-bit elements; how exact they have to be, the bound alone decides.
A program may use at most 64 MiB of HBM per device.

v0:
```python
import jax
import jax.numpy as jnp
import numpy as np
from jax import lax
from jax.sharding import PartitionSpec as P


def in_blocks(array, dim, count):
    shape = array.shape
    parts = array.reshape(*shape[:dim], count, shape[dim] // count, *shape[dim + 1 :])
    return jnp.moveaxis(parts, dim, 0)


def summed_on_arrival(array, axis, dim):
    count = lax.axis_size(axis)
    parts = lax.all_to_all(in_blocks(array, dim, count), axis, 0, 0, tiled=True)
    return jnp.sum(parts, axis=0)


def lookup(indices, values_table):
    positions = jnp.arange(values_table.shape[0], dtype=jnp.int32)
    picked = jnp.where(indices[:, None] == positions[None, :], values_table[None, :], 0.0)
    return jnp.sum(picked, axis=1)


def owner_blocks(partial_sum):
    col_count = lax.axis_size("col")
    layer_count = lax.axis_size("layer")
    pair_rows = partial_sum.shape[0] // col_count
    slab_cols = partial_sum.shape[1] // layer_count
    blocks = partial_sum.reshape(col_count, pair_rows, layer_count, slab_cols)
    return blocks.transpose(0, 2, 1, 3).reshape(col_count * layer_count * pair_rows, slab_cols)


def shards(amplitudes, integrals, occ_energy, vir_energy):
    partial_rows = jnp.dot(
        amplitudes,
        lax.all_gather(integrals, "row", axis=1, tiled=True),
        precision=lax.Precision.HIGHEST,
        preferred_element_type=jnp.float32,
    )
    partial_sum = lax.all_to_all(partial_rows, "row", split_axis=1, concat_axis=0, tiled=True)
    ladder = summed_on_arrival(owner_blocks(partial_sum), ("col", "layer"), 0)
    pair_rows = ladder.shape[0]
    slab_cols = ladder.shape[1]
    occupied = occ_energy.shape[0]
    virtuals = vir_energy.shape[0]
    first_np, second_np = np.triu_indices(occupied, 1)
    ij_start = lax.axis_index("col") * pair_rows
    ab_start = (
        lax.axis_index("row") * lax.axis_size("layer") + lax.axis_index("layer")
    ) * slab_cols
    first_index = lax.dynamic_slice_in_dim(
        jnp.asarray(first_np, dtype=jnp.int32), ij_start, pair_rows
    )
    second_index = lax.dynamic_slice_in_dim(
        jnp.asarray(second_np, dtype=jnp.int32), ij_start, pair_rows
    )
    pair_sum = lookup(first_index, occ_energy) + lookup(second_index, occ_energy)
    ab_index = ab_start + jnp.arange(slab_cols, dtype=jnp.int32)
    vir_sum = lookup(ab_index // virtuals, vir_energy) + lookup(ab_index % virtuals, vir_energy)
    denominator = pair_sum[:, None] - vir_sum[None, :]
    return (ladder, ladder / denominator)


def solution(mesh):
    in_specs = (P("row", ("layer", "col")), P(("layer", "col"), "row"), P(), P())
    out_specs = (P("col", ("row", "layer")), P("col", ("row", "layer")))
    return jax.shard_map(shards, mesh=mesh, in_specs=in_specs, out_specs=out_specs, check_vma=False)
```

profile of v0, /device:TPU:2, one launch (start us, length us, event | category | flops | bytes accessed | tf_op | source)
XLA Modules:
  0.0 188.2 jit_solution(8743574905029735897)
XLA Ops:
  7.2 0.0 copy-start
  7.2 0.0 all-gather.2.cloned.1.call-start
  7.2 0.7 all-gather.2.cloned.1.call-update
  7.9 64.1 %all-gather.2.cloned.1.call-done = f32[1149,768]{0,1:T(8,128)} async-done(((f32[1149,192]{0,1:T(8,128)}), f32[1149,768]{0,1:T(8,128)}) %all-gather.2.cloned.1.call-update) | async-done | bytes 3529744 | tf_op jit(solution)/shard_map/all_gather | solution.py:38
  72.0 0.0 copy-done
  72.0 8.3 %fusion.1 = f32[504,768]{0,1:T(8,128)S(1)} fusion(f32[504,1149]{1,0:T(8,128)S(1)} %copy-done, f32[1149,768]{0,1:T(8,128)} %all-gather.2.cloned.1.call-done), kind=kOutput, calls=%fused_computation.13 | convolution fusion | flops 5336948736 | bytes 7394400 | tf_op jit(solution)/shard_map/dot_general | solution.py:36
  80.3 35.7 %all_to_all.21 = f32[504,4,192]{0,2,1:T(8,128)S(1)} all-to-all(f32[504,4,192]{0,2,1:T(8,128)S(1)} %bitcast.11), channel_id=1, replica_groups=mesh['row'=4,'col'=16,'layer'=4] {'row'}, dimensions={1} | all-to-all | bytes 3096576 | tf_op jit(solution)/shard_map/all_to_all | solution.py:42
  116.0 2.2 %copy.12 = f32[4,504,192]{1,0,2:T(4,128)} copy(f32[4,504,192]{1,2,0:T(8,128)S(1)} %bitcast.9) | data formatting | bytes 3096576 | tf_op jit(solution)/shard_map/all_to_all | solution.py:42
  118.2 2.9 %reshape.43 = f32[16,126,4,48]{1,0,3,2:T(8,128)} reshape(f32[4,504,192]{1,0,2:T(4,128)} %copy.12) | data formatting | bytes 3096576 | tf_op jit(solution)/shard_map/reshape | solution.py:31
  121.1 3.1 %copy.13 = f32[16,4,126,48]{2,3,1,0:T(8,128)} copy(f32[16,4,126,48]{2,0,3,1:T(8,128)} %bitcast.10) | data formatting | bytes 3096576 | tf_op jit(solution)/shard_map/transpose | solution.py:32
  124.2 0.0 copy-start.2
  124.2 0.0 copy-start.3
  124.2 16.2 %all-to-all-start.1 = ((f32[64,126,48]{1,2,0:T(8,128)}), f32[64,126,48]{1,2,0:T(8,128)}, u32[]{:S(2)}, u32[]{:S(2)}) async-start(f32[64,126,48]{1,2,0:T(8,128)} %bitcast.8), calls=%async_computation.1 | async-start | bytes 3145728 | tf_op jit(solution)/shard_map/all_to_all | solution.py:16
  140.4 0.8 dynamic_slice.7
  141.2 0.8 dynamic_slice.6
  142.0 0.0 copy-done.2
  142.0 0.2 select_reduce_fusion
  142.2 0.0 copy-done.3
  142.2 0.1 select_reduce_fusion.2
  142.3 36.7 %all-to-all-done.1 = f32[64,126,48]{1,2,0:T(8,128)} async-done(((f32[64,126,48]{1,2,0:T(8,128)}), f32[64,126,48]{1,2,0:T(8,128)}, u32[]{:S(2)}, u32[]{:S(2)}) %all-to-all-start.1) | async-done | bytes 1548320 | tf_op jit(solution)/shard_map/all_to_all | solution.py:16
  179.1 1.6 reduce_sum.45
  180.6 0.0 copy-start.1
  180.6 0.7 subtract_divide_fusion
  181.3 0.0 copy-done.1
  (3 shorter events, 0.0 us)
Async XLA Ops:
  7.2 64.9 %copy-start = (f32[504,1149]{1,0:T(8,128)S(1)}, f32[504,1149]{1,0:T(8,128)}, u32[]{:S(2)}) copy-start(f32[504,1149]{1,0:T(8,128)} %param.6) | copy-start | bytes 6949156
  7.2 64.8 %all-gather.2.cloned.1.call-start = ((), (), s32[]{:S(2)}) async-start(), calls=%async_computation.2 | async-start | bytes 4423680 | tf_op jit(solution)/shard_map/all_gather | solution.py:38
  124.2 17.8 %copy-start.2 = (f32[384]{0:T(512)S(1)}, f32[384]{0:T(512)}, u32[]{:S(2)}) copy-start(f32[384]{0:T(512)} %param.9) | copy-start | bytes 4612
  124.2 18.0 %copy-start.3 = (f32[64]{0:T(128)S(1)}, f32[64]{0:T(128)}, u32[]{:S(2)}) copy-start(f32[64]{0:T(128)} %param.8) | copy-start | bytes 772
  124.2 54.9 %all-to-all-start.1 = ((f32[64,126,48]{1,2,0:T(8,128)}), f32[64,126,48]{1,2,0:T(8,128)}, u32[]{:S(2)}, u32[]{:S(2)}) async-start(f32[64,126,48]{1,2,0:T(8,128)} %bitcast.8), calls=%async_computation.1 | async-start | bytes 3145728 | tf_op jit(solution)/shard_map/all_to_all | solution.py:16
  180.6 0.7 copy-start.1
Sparse Core Ops, SparseCore 0:
  9.8 62.1 all-gather.1
where the time goes:
time: 189 us; the launch traced here: 188 us
  waiting for transfers between devices  102 us (54%)
  blocking collectives  35.7 us (19%)
  starting transfers between devices  16.3 us (9%)
  between operations  14.1 us (7%)
  local copies, waits for them, and re-layouts  9.7 us (5%)
  matrix products  8.3 us (4%)
  other arithmetic  2.55 us (1%)
    all_gather x1, waiting for transfers between devices, shards(): lax.all_gather(integrals, 'row', axis=1, tiled=True)  64.1 us
    all_to_all x1, waiting for transfers between devices, summed_on_arrival(): parts = lax.all_to_all(in_blocks(array, dim, count), axis, 0, 0, tiled=True)  36.7 us
    all_to_all x1, blocking collectives, shards(): lax.all_to_all(partial_rows, 'row', split_axis=1, concat_axis=0, tiled=True)  35.7 us
    all_to_all x1, starting transfers between devices, summed_on_arrival(): parts = lax.all_to_all(in_blocks(array, dim, count), axis, 0, 0, tiled=True)  16.2 us
    dot_general x1, matrix products, shards(): jnp.dot(amplitudes, lax.all_gather(integrals, 'row', axis=1, tiled=True),...  8.3 us
  transfers between devices with their start and end apart: 2, of which 2 were waited for; matrix products, arithmetic and copies ran while one was open for 1% of the time, Pallas kernels for 0%

commit v1 on v0

--- a/solution.py
+++ b/solution.py
@@ -35,7 +35,9 @@
 def shards(amplitudes, integrals, occ_energy, vir_energy):
     partial_rows = jnp.dot(
         amplitudes,
-        lax.all_gather(integrals, "row", axis=1, tiled=True),
+        jnp.concatenate(
+            lax.all_to_all(jnp.stack([integrals] * lax.axis_size("row")), "row", 0, 0), axis=1
+        ),
         precision=lax.Precision.HIGHEST,
         preferred_element_type=jnp.float32,
     )

time: 189 us -> 201 us (1.063)
  blocking collectives: 35.7 us -> 133 us
  waiting for transfers between devices: 102 us -> 36.7 us
  between operations: 14.1 us -> 0.7 us
  starting transfers between devices: 16.3 us -> 9.95 us
    all_to_all x0 -> x1, blocking collectives: none -> 90.7 us  [shards(): lax.all_to_all(jnp.stack([integrals] * lax.axis_size('row')), 'row', 0, 0)]
    all_gather x1 -> x0, waiting for transfers between devices: 64.1 us -> none  [shards(): lax.all_gather(integrals, 'row', axis=1, tiled=True)]
    all_to_all x1, blocking collectives: 35.7 us -> 42.6 us  [shards(): lax.all_to_all(partial_rows, 'row', split_axis=1, concat_axis=0, tiled=True)]
    all_to_all x1, starting transfers between devices: 16.2 us -> 9.95 us  [summed_on_arrival(): parts = lax.all_to_all(in_blocks(array, dim, count), axis, 0, 0, tiled=True)]
  transfers between devices with their start and end apart: 2 -> 1, of which waited for: 2 -> 1; matrix products, arithmetic and copies ran while one was open for 1% -> 1% of each run, Pallas kernels for 0% -> 0%
where the time goes in v1:
time: 201 us
  blocking collectives  133 us (66%)
  waiting for transfers between devices  36.7 us (18%)
  local copies, waits for them, and re-layouts  11.2 us (6%)
  starting transfers between devices  9.95 us (5%)
  matrix products  6.4 us (3%)
  other arithmetic  2.55 us (1%)
    all_to_all x1, blocking collectives, shards(): lax.all_to_all(jnp.stack([integrals] * lax.axis_size('row')), 'row', 0, 0)  90.7 us
    all_to_all x1, blocking collectives, shards(): lax.all_to_all(partial_rows, 'row', split_axis=1, concat_axis=0, tiled=True)  42.6 us
    all_to_all x1, waiting for transfers between devices, summed_on_arrival(): parts = lax.all_to_all(in_blocks(array, dim, count), axis, 0, 0, tiled=True)  36.7 us
    all_to_all x1, starting transfers between devices, summed_on_arrival(): parts = lax.all_to_all(in_blocks(array, dim, count), axis, 0, 0, tiled=True)  9.95 us
    dot_general x1, matrix products, shards(): jnp.dot(amplitudes, jnp.concatenate(lax.all_to_all(jnp.stack([integrals]...  6.4 us
  transfers between devices with their start and end apart: 1, of which 1 were waited for; matrix products, arithmetic and copies ran while one was open for 1% of the time, Pallas kernels for 0%

profile of v1, /device:TPU:2, one launch (start us, length us, event | category | flops | bytes accessed | tf_op | source)
XLA Modules:
  0.0 200.9 jit_solution(1172027387834108615)
XLA Ops:
  0.6 0.0 copy-start
  0.6 1.5 stack.2
  2.2 90.7 %all_to_all.23 = f32[4,1149,192]{1,2,0:T(8,128)S(1)} all-to-all(f32[4,1149,192]{1,2,0:T(8,128)S(1)} %stack.2), channel_id=1, replica_groups=mesh['row'=4,'col'=16,'layer'=4] {'row'}, dimensions={0} | all-to-all | bytes 7059456 | tf_op jit(solution)/shard_map/all_to_all | solution.py:39
  92.8 0.0 copy-done
  92.8 6.4 %fusion = f32[504,4,192]{0,2,1:T(8,128)S(1)} fusion(f32[4,1149,192]{1,2,0:T(8,128)S(1)} %all_to_all.23, f32[504,1149]{1,0:T(8,128)S(1)} %copy-done), kind=kOutput, calls=%fused_computation | convolution fusion | flops 5336948736 | bytes 7394400 | tf_op jit(solution)/shard_map/dot_general | solution.py:36
  99.3 42.6 %all_to_all.24 = f32[504,4,192]{0,2,1:T(8,128)S(1)} all-to-all(f32[504,4,192]{0,2,1:T(8,128)S(1)} %fusion), channel_id=1, replica_groups=mesh['row'=4,'col'=16,'layer'=4] {'row'}, dimensions={1} | all-to-all | bytes 3096576 | tf_op jit(solution)/shard_map/all_to_all | solution.py:44
  141.9 2.2 %copy.10 = f32[4,504,192]{1,0,2:T(4,128)} copy(f32[4,504,192]{1,2,0:T(8,128)S(1)} %bitcast.18) | data formatting | bytes 3096576 | tf_op jit(solution)/shard_map/all_to_all | solution.py:44
  144.1 2.9 %reshape.54 = f32[16,126,4,48]{1,0,3,2:T(8,128)} reshape(f32[4,504,192]{1,0,2:T(4,128)} %copy.10) | data formatting | bytes 3096576 | tf_op jit(solution)/shard_map/reshape | solution.py:31
  147.0 3.1 %copy.11 = f32[16,4,126,48]{2,3,1,0:T(8,128)} copy(f32[16,4,126,48]{2,0,3,1:T(8,128)} %bitcast.19) | data formatting | bytes 3096576 | tf_op jit(solution)/shard_map/transpose | solution.py:32
  150.0 0.0 copy-start.2
  150.0 0.0 copy-start.3
  150.0 9.9 %all-to-all-start.2 = ((f32[64,126,48]{1,2,0:T(8,128)}), f32[64,126,48]{1,2,0:T(8,128)}, u32[]{:S(2)}, u32[]{:S(2)}) async-start(f32[64,126,48]{1,2,0:T(8,128)} %bitcast.17), calls=%async_computation.2 | async-start | bytes 3145728 | tf_op jit(solution)/shard_map/all_to_all | solution.py:16
  160.0 0.8 dynamic_slice.7
  160.8 0.8 dynamic_slice.6
  161.6 0.0 copy-done.2
  161.6 0.2 select_reduce_fusion
  161.8 0.0 copy-done.3
  161.8 0.1 select_reduce_fusion.2
  161.9 36.7 %all-to-all-done.2 = f32[64,126,48]{1,2,0:T(8,128)} async-done(((f32[64,126,48]{1,2,0:T(8,128)}), f32[64,126,48]{1,2,0:T(8,128)}, u32[]{:S(2)}, u32[]{:S(2)}) %all-to-all-start.2) | async-done | bytes 1548320 | tf_op jit(solution)/shard_map/all_to_all | solution.py:16
  198.6 1.6 reduce_sum.45
  200.2 0.0 copy-start.1
  200.2 0.7 subtract_divide_fusion
  200.9 0.0 copy-done.1
  (3 shorter events, 0.0 us)
Async XLA Ops:
  0.6 92.2 %copy-start = (f32[504,1149]{1,0:T(8,128)S(1)}, f32[504,1149]{1,0:T(8,128)}, u32[]{:S(2)}) copy-start(f32[504,1149]{1,0:T(8,128)} %param.6) | copy-start | bytes 6949156
  150.0 11.5 %copy-start.2 = (f32[384]{0:T(512)S(1)}, f32[384]{0:T(512)}, u32[]{:S(2)}) copy-start(f32[384]{0:T(512)} %param.9) | copy-start | bytes 4612
  150.0 11.7 %copy-start.3 = (f32[64]{0:T(128)S(1)}, f32[64]{0:T(128)}, u32[]{:S(2)}) copy-start(f32[64]{0:T(128)} %param.8) | copy-start | bytes 772
  150.0 48.6 %all-to-all-start.2 = ((f32[64,126,48]{1,2,0:T(8,128)}), f32[64,126,48]{1,2,0:T(8,128)}, u32[]{:S(2)}, u32[]{:S(2)}) async-start(f32[64,126,48]{1,2,0:T(8,128)} %bitcast.17), calls=%async_computation.2 | async-start | bytes 3145728 | tf_op jit(solution)/shard_map/all_to_all | solution.py:16
  200.2 0.7 copy-start.1
